TPU v7x, 32 devices: a whole 2x2x4 slice. The times are simulated.
32 devices in a mesh: dp: 8 (over y, x, core), mp: 4 (over z).
Axes of the slice: x: 2, y: 2, z: 4, core: 2. Of those that a mesh axis runs over, the one named last changes fastest.
Arguments:
- candidates: bfloat16 [64, 256, 768], P('dp', 'mp'), may hold values from -6 to 6
- owner_row: int32 [64], replicated, may hold values from 0 to 63, as said below
- selected: int32 [16], replicated, may hold values from 0 to 63, as said below
- dest_slot: int32 [16], replicated, may hold values from 0 to 15, as said below
- patch_weight: bfloat16 [768, 768], P(None, 'mp'), may hold values from -0.21875 to 0.21875
- positions: bfloat16 [256, 768], P(None, 'mp'), may hold values from -3 to 3
- qkv_weight: bfloat16 [768, 3, 768], P(None, None, 'mp'), may hold values from -1 to 1
- out_weight: bfloat16 [768, 768], P('mp'), may hold values from -0.21875 to 0.21875
- attn_gain: bfloat16 [768], replicated, may hold values from 0.099609375 to 1.8984375
- mlp_gain: bfloat16 [768], replicated, may hold values from 0.099609375 to 1.8984375
- up_weight: bfloat16 [768, 3072], P(None, 'mp'), may hold values from -0.21875 to 0.21875
- down_weight: bfloat16 [3072, 768], P('mp'), may hold values from -0.109375 to 0.109375
Outputs:
- layer_out: bfloat16 [16, 256, 768], P('dp', 'mp')
Inputs may be any that keep to these rules, and one draw needn't show every extreme that they name: `owner_row`: a permutation; storage row r sits on index r // 8 of dp. `selected`: distinct candidates; no index of dp stores more than 4 of them, and some index stores exactly 4. `dest_slot`: a permutation; the 2 slots s with equal s // 2 get candidates stored on different indices of dp.
All inputs are finite; a program needn't handle non-finite values.
Results may differ from a plain program's by a relative error of at most 0.012.
Values may be sent and summed in bfloat16 or wider, within the bound.
No kernel may reach another device: no remote copies, remote signals or barrier semaphores. Data moves between devices by JAX's collectives and lax.ppermute only.
A program may use at most 128 MiB of HBM per device.

v0:
```python
import jax
import jax.numpy as jnp
from jax import lax
from jax.sharding import PartitionSpec as P

PATCHES = 256
CAND_DEV = 8
SEL_DEV = 2
HEAD_DIM = 64


def norm_rows(values, gain):
    average = jnp.mean(values, axis=-1, keepdims=True)
    centred = values - average
    variance = jnp.mean(centred * centred, axis=-1, keepdims=True)
    return centred * lax.rsqrt(variance + 1e-06) * gain.astype(jnp.float32)


def local(
    candidates,
    owner_row,
    selected,
    dest_slot,
    patch_weight,
    positions,
    qkv_weight,
    out_weight,
    attn_gain,
    mlp_gain,
    up_weight,
    down_weight,
):
    learners = lax.axis_size("dp")
    own_index = lax.axis_index("dp")
    quarter = candidates.shape[1]
    pixel_width = candidates.shape[2]
    chosen_rows = jnp.take(owner_row, selected)
    slot_rows = jnp.zeros(dest_slot.shape, jnp.int32).at[dest_slot].set(chosen_rows)
    source_owner = slot_rows // CAND_DEV
    local_row = slot_rows % CAND_DEV
    stored = candidates.reshape(CAND_DEV, quarter * pixel_width)
    mine = (source_owner == own_index).reshape(learners, SEL_DEV)
    picked = jnp.sum(jnp.where(mine, local_row.reshape(learners, SEL_DEV), 0), axis=1)
    outgoing = jnp.take(stored, picked, axis=0)
    incoming = lax.all_to_all(outgoing, "dp", split_axis=0, concat_axis=0, tiled=True)
    senders = lax.dynamic_slice_in_dim(source_owner, own_index * SEL_DEV, SEL_DEV)
    arrived = jnp.take(incoming, senders, axis=0)
    own_pixels = arrived.reshape(SEL_DEV, quarter, pixel_width)
    product = jnp.einsum(
        "brp,pe->bre",
        lax.all_gather(own_pixels, "mp", axis=1, tiled=True),
        patch_weight,
        preferred_element_type=jnp.float32,
    )
    embedded = (product + positions.astype(jnp.float32)[None]).astype(jnp.bfloat16)
    activations = lax.all_gather(embedded, "mp", axis=2, tiled=True).astype(jnp.float32)
    normed = norm_rows(activations, attn_gain).astype(jnp.bfloat16)
    projected = jnp.einsum(
        "btd,dce->btce", normed, qkv_weight, preferred_element_type=jnp.float32
    ).astype(jnp.bfloat16)
    local_heads = qkv_weight.shape[2] // HEAD_DIM
    head_split = projected.reshape(SEL_DEV, PATCHES, 3, local_heads, HEAD_DIM)
    queries = head_split[:, :, 0]
    attn_keys = head_split[:, :, 1]
    attn_values = head_split[:, :, 2]
    scores = jnp.einsum(
        "bqhd,bkhd->bhqk", queries, attn_keys, preferred_element_type=jnp.float32
    ) * HEAD_DIM ** (-0.5)
    attn_probs = jax.nn.softmax(scores, axis=-1).astype(jnp.bfloat16)
    context = jnp.einsum(
        "bhqk,bkhd->bqhd", attn_probs, attn_values, preferred_element_type=jnp.float32
    ).astype(jnp.bfloat16)
    context = context.reshape(SEL_DEV, PATCHES, local_heads * HEAD_DIM)
    partial_out = jnp.einsum("bte,ed->btd", context, out_weight, preferred_element_type=jnp.float32)
    attended = lax.psum(partial_out.astype(jnp.bfloat16), "mp").astype(jnp.float32)
    after_attn = activations + attended
    normed2 = norm_rows(after_attn, mlp_gain).astype(jnp.bfloat16)
    hidden = jax.nn.gelu(
        jnp.einsum("btd,df->btf", normed2, up_weight, preferred_element_type=jnp.float32),
        approximate=False,
    ).astype(jnp.bfloat16)
    down_terms = jnp.einsum("btf,fd->btd", hidden, down_weight, preferred_element_type=jnp.float32)
    summed = lax.psum_scatter(
        down_terms.astype(jnp.bfloat16), "mp", scatter_dimension=1, tiled=True
    ).astype(jnp.float32)
    residual = lax.dynamic_slice_in_dim(after_attn, lax.axis_index("mp") * quarter, quarter, 1)
    return (residual + summed).astype(jnp.bfloat16)


def solution(mesh):
    return jax.shard_map(
        local,
        mesh=mesh,
        in_specs=(
            P("dp", "mp", None),
            P(),
            P(),
            P(),
            P(None, "mp"),
            P(None, "mp"),
            P(None, None, "mp"),
            P("mp", None),
            P(),
            P(),
            P(None, "mp"),
            P("mp", None),
        ),
        out_specs=P("dp", "mp", None),
        check_vma=False,
    )
```

profile of v0, /device:TPU:0, one launch (start us, length us, event | category | flops | bytes accessed | tf_op | source)
XLA Modules:
  0.0 183.8 jit_solution(13271876456663978697)
XLA Ops:
  6.5 0.8 compare_select_fusion.3
  7.3 1.3 gather_fusion
  10.2 1.6 copy.77
  11.8 1.1 gather_fusion.1
  13.5 1.2 reduce.4
  14.7 1.5 reshape.149
  16.2 5.2 %all-to-all-start = ((bf16[8,2,24576]{2,1,0:T(2,128)(2,1)}), bf16[8,2,24576]{2,1,0:T(2,128)(2,1)S(1)}, u32[]{:S(2)}, u32[]{:S(2)}) async-start(bf16[8,2,24576]{2,1,0:T(2,128)(2,1)} %reshape.149), calls=%async_computation | async-start | bytes 1572864 | tf_op jit(solution)/shard_map/all_to_all | solution.py:45
  22.3 11.7 %all-to-all-done = bf16[8,2,24576]{2,1,0:T(2,128)(2,1)S(1)} async-done(((bf16[8,2,24576]{2,1,0:T(2,128)(2,1)}), bf16[8,2,24576]{2,1,0:T(2,128)(2,1)S(1)}, u32[]{:S(2)}, u32[]{:S(2)}) %all-to-all-start) | async-done | bytes 786464 | tf_op jit(solution)/shard_map/all_to_all | solution.py:45
  34.0 0.8 reshape.150
  34.8 0.9 copy.82
  35.7 0.8 gather_fusion.2
  36.6 18.1 %all_gather.6 = bf16[2,256,768]{2,1,0:T(8,128)(2,1)S(1)} all-gather(bf16[2,64,768]{2,1,0:T(8,128)(2,1)S(1)} %bitcast_select_fusion.1), channel_id=1, replica_groups=mesh['dp'=8,'mp'=4] {'mp'}, dimensions={1}, use_global_device_ids=true | all-gather | bytes 983040 | tf_op jit(solution)/shard_map/all_gather | solution.py:51
  55.3 17.4 %all_gather.7 = bf16[2,256,768]{1,0,2:T(2,128)(2,1)S(1)} all-gather(bf16[2,256,192]{1,0,2:T(2,128)(2,1)S(1)} %copy.63), channel_id=1, replica_groups=mesh['dp'=8,'mp'=4] {'mp'}, dimensions={2}, use_global_device_ids=true | all-gather | bytes 983040 | tf_op jit(solution)/shard_map/all_gather | solution.py:56
  74.5 0.8 convolution_convert_fusion.2
  76.0 0.9 convolution_convert_fusion.3
  76.9 1.3 convolution_convert_fusion.1
  78.5 44.0 %all-reduce.4.cloned.1.call-done = bf16[2,256,768]{2,1,0:T(8,128)(2,1)} async-done(((bf16[2,256,768]{2,1,0:T(8,128)(2,1)}), bf16[2,256,768]{2,1,0:T(8,128)(2,1)}) %all-reduce.4.cloned.1.call-update) | async-done | bytes 786448 | tf_op jit(solution)/shard_map/psum | solution.py:75
  122.5 1.5 fusion.107
  124.5 1.3 fusion.63
  125.7 4.4 %convolution_convert_fusion = bf16[2,256,768]{2,1,0:T(8,128)(2,1)S(1)} fusion(bf16[768,768]{1,0:T(8,128)(2,1)S(1)} %copy-done.8, f32[2,256,768]{2,1,0:T(8,128)S(1)} %get-tuple-element.13, u8[256,768]{1,0:T(8,128)(4,1)S(1)} %get-tuple-element.6, u8[256,768]{1,0:T(8,128)(4,1)S(1)} %get-tuple-element.5), kind=kOutput, calls=%fused_computation.41 | convolution fusion | flops 631898112 | bytes 3932160 | tf_op jit(solution)/shard_map/btf,fd->btd/dot_general | solution.py:82
  130.2 1.7 copy.69
  133.2 42.0 %all-reduce.6.cloned.1.call-done = bf16[2,256,768]{2,0,1:T(2,128)(2,1)} async-done(((bf16[2,256,768]{2,0,1:T(2,128)(2,1)}), bf16[2,256,768]{2,0,1:T(2,128)(2,1)}) %all-reduce.6.cloned.1.call-update) | async-done | bytes 786448
  175.2 1.1 constant_dynamic-slice_fusion
  176.3 0.7 add_convert_fusion
  (55 shorter events, 7.5 us)
Async XLA Ops:
  6.5 117.9 %copy-start = (bf16[768,768]{1,0:T(8,128)(2,1)S(1)}, bf16[768,768]{1,0:T(8,128)(2,1)}, u32[]{:S(2)}) copy-start(bf16[768,768]{1,0:T(8,128)(2,1)} %param.22) | copy-start | bytes 3538948
  14.7 6.8 %copy-start.5 = (bf16[256,192]{0,1:T(8,128)(2,1)S(1)}, bf16[256,192]{0,1:T(8,128)(2,1)}, u32[]{:S(2)}) copy-start(bf16[256,192]{0,1:T(8,128)(2,1)} %param.17) | copy-start | bytes 294916
  14.7 7.5 %copy-start.6 = (bf16[768]{0:T(1024)(128)(2,1)S(1)}, bf16[768]{0:T(1024)(128)(2,1)}, u32[]{:S(2)}) copy-start(bf16[768]{0:T(1024)(128)(2,1)} %param.20) | copy-start | bytes 4612
  16.2 17.8 %all-to-all-start = ((bf16[8,2,24576]{2,1,0:T(2,128)(2,1)}), bf16[8,2,24576]{2,1,0:T(2,128)(2,1)S(1)}, u32[]{:S(2)}, u32[]{:S(2)}) async-start(bf16[8,2,24576]{2,1,0:T(2,128)(2,1)} %reshape.149), calls=%async_computation | async-start | bytes 1572864 | tf_op jit(solution)/shard_map/all_to_all | solution.py:45
  21.4 101.1 %all-reduce.4.cloned.1.call-start = ((), (), s32[]{:S(2)}) async-start(), calls=%async_computation.1 | async-start | bytes 1572864 | tf_op jit(solution)/shard_map/psum | solution.py:75
  35.7 19.0 %copy-start.2 = (f32[256,192]{0,1:T(8,128)S(1)}, f32[256,192]{0,1:T(8,128)}, u32[]{:S(2)}) copy-start(f32[256,192]{0,1:T(8,128)} %convert_element_type.51) | copy-start | bytes 589828
  35.7 19.0 %copy-start.4 = (bf16[768,192]{0,1:T(8,128)(2,1)S(1)}, bf16[768,192]{0,1:T(8,128)(2,1)}, u32[]{:S(2)}) copy-start(bf16[768,192]{0,1:T(8,128)(2,1)} %param.16) | copy-start | bytes 884740
  73.3 1.2 copy-start.9
  76.0 1.0 copy-start.3
  76.9 1.6 copy-start.7
  78.3 96.9 %all-reduce.6.cloned.1.call-start = ((), (), s32[]{:S(2)}) async-start(), calls=%async_computation.2 | async-start | bytes 1572864
  122.5 1.5 copy-start.1
  124.4 1.3 copy-start.8
  130.2 1.8 copy-start.10
Sparse Core Ops, SparseCore 0:
  78.4 44.0 all-reduce.3
  132.0 43.1 all-reduce.5
where the time goes:
time: 184 us
  waiting for transfers between devices  97.8 us (53%)
  blocking collectives  35.5 us (19%)
  between operations  14.3 us (8%)
  local copies, waits for them, and re-layouts  14 us (8%)
  matrix products  9.79 us (5%)
  other arithmetic  7.02 us (4%)
  starting transfers between devices  5.46 us (3%)
    psum x1, waiting for transfers between devices, local(): lax.psum(partial_out.astype(jnp.bfloat16), 'mp').astype(jnp.float32)  44 us
    unnamed x3, waiting for transfers between devices  42.1 us
    all_gather x1, blocking collectives, local(): lax.all_gather(own_pixels, 'mp', axis=1, tiled=True)  18.1 us
    all_gather x1, blocking collectives, local(): lax.all_gather(embedded, 'mp', axis=2, tiled=True).astype(jnp.float32)  17.4 us
    all_to_all x1, waiting for transfers between devices, local(): lax.all_to_all(outgoing, 'dp', split_axis=0, concat_axis=0, tiled=True)  11.7 us
    unnamed x28, local copies, waits for them, and re-layouts  7.11 us
    all_to_all x1, starting transfers between devices, local(): lax.all_to_all(outgoing, 'dp', split_axis=0, concat_axis=0, tiled=True)  5.2 us
    dot_general x1, matrix products, local(): jnp.einsum('btf,fd->btd', hidden, down_weight, preferred_element_type=jnp...  4.43 us
  transfers between devices with their start and end apart: 3, of which 3 were waited for; matrix products, arithmetic and copies ran while one was open for 1% of the time, Pallas kernels for 0%

commit v1 on v0

--- a/solution.py
+++ b/solution.py
@@ -48,7 +48,15 @@
     own_pixels = arrived.reshape(SEL_DEV, quarter, pixel_width)
     product = jnp.einsum(
         "brp,pe->bre",
-        lax.all_gather(own_pixels, "mp", axis=1, tiled=True),
+        jnp.concatenate(
+            lax.all_to_all(
+                jnp.stack(lax.axis_size("mp") * [own_pixels], 0),
+                axis_name="mp",
+                split_axis=0,
+                concat_axis=0,
+            ),
+            axis=1,
+        ),
         patch_weight,
         preferred_element_type=jnp.float32,
     )

time: 184 us -> 190 us (1.033)
  waiting for transfers between devices: 97.8 us -> 116 us
  blocking collectives: 35.5 us -> 17.7 us
  starting transfers between devices: 5.46 us -> 10.4 us
    all_gather x1 -> x0, blocking collectives: 18.1 us -> none  [local(): lax.all_gather(own_pixels, 'mp', axis=1, tiled=True)]
    all_to_all x0 -> x1, waiting for transfers between devices: none -> 17.3 us  [local(): lax.all_to_all(jnp.stack(lax.axis_size('mp') * [own_pixels], 0), axis_nam...]
    all_to_all x0 -> x1, starting transfers between devices: none -> 5 us  [local(): lax.all_to_all(jnp.stack(lax.axis_size('mp') * [own_pixels], 0), axis_nam...]
    unnamed x28 -> x26, local copies, waits for them, and re-layouts: 7.11 us -> 7.1 us
  transfers between devices with their start and end apart: 3 -> 4, of which waited for: 3 -> 4; matrix products, arithmetic and copies ran while one was open for 1% -> 0% of each run, Pallas kernels for 0% -> 0%
where the time goes in v1:
time: 190 us
  waiting for transfers between devices  116 us (61%)
  blocking collectives  17.7 us (9%)
  local copies, waits for them, and re-layouts  15 us (8%)
  between operations  14.3 us (8%)
  starting transfers between devices  10.4 us (5%)
  matrix products  9.78 us (5%)
  other arithmetic  6.35 us (3%)
    psum x1, waiting for transfers between devices, local(): lax.psum(partial_out.astype(jnp.bfloat16), 'mp').astype(jnp.float32)  44.4 us
    unnamed x3, waiting for transfers between devices  42.1 us
    all_gather x1, blocking collectives, local(): lax.all_gather(embedded, 'mp', axis=2, tiled=True).astype(jnp.float32)  17.7 us
    all_to_all x1, waiting for transfers between devices, local(): lax.all_to_all(jnp.stack(lax.axis_size('mp') * [own_pixels], 0), axis_nam...  17.3 us
    all_to_all x1, waiting for transfers between devices, local(): lax.all_to_all(outgoing, 'dp', split_axis=0, concat_axis=0, tiled=True)  12.5 us
    unnamed x26, local copies, waits for them, and re-layouts  7.1 us
    all_to_all x1, starting transfers between devices, local(): lax.all_to_all(outgoing, 'dp', split_axis=0, concat_axis=0, tiled=True)  5.2 us
    all_to_all x1, starting transfers between devices, local(): lax.all_to_all(jnp.stack(lax.axis_size('mp') * [own_pixels], 0), axis_nam...  5 us
  transfers between devices with their start and end apart: 4, of which 4 were waited for; matrix products, arithmetic and copies ran while one was open for 0% of the time, Pallas kernels for 0%

profile of v1, /device:TPU:0, one launch (start us, length us, event | category | flops | bytes accessed | tf_op | source)
XLA Modules:
  0.0 189.8 jit_solution(10244595845617814187)
XLA Ops:
  7.3 1.3 gather_fusion
  10.2 1.6 copy.81
  11.8 1.1 gather_fusion.1
  13.5 1.2 reduce.4
  14.7 1.5 reshape.161
  16.2 5.2 %all-to-all-start = ((bf16[8,2,24576]{2,1,0:T(2,128)(2,1)}), bf16[8,2,24576]{2,1,0:T(2,128)(2,1)S(1)}, u32[]{:S(2)}, u32[]{:S(2)}) async-start(bf16[8,2,24576]{2,1,0:T(2,128)(2,1)} %reshape.161), calls=%async_computation | async-start | bytes 1572864 | tf_op jit(solution)/shard_map/all_to_all | solution.py:45
  21.5 12.5 %all-to-all-done = bf16[8,2,24576]{2,1,0:T(2,128)(2,1)S(1)} async-done(((bf16[8,2,24576]{2,1,0:T(2,128)(2,1)}), bf16[8,2,24576]{2,1,0:T(2,128)(2,1)S(1)}, u32[]{:S(2)}, u32[]{:S(2)}) %all-to-all-start) | async-done | bytes 786464 | tf_op jit(solution)/shard_map/all_to_all | solution.py:45
  34.0 0.8 reshape.162
  34.8 0.9 copy.86
  35.7 0.8 gather_fusion.2
  36.6 0.9 stack.3
  37.5 5.0 %all-to-all-start.1 = ((bf16[4,2,64,768]{3,2,1,0:T(8,128)(2,1)}), bf16[4,2,64,768]{3,2,1,0:T(8,128)(2,1)S(1)}, u32[]{:S(2)}, u32[]{:S(2)}) async-start(bf16[4,2,64,768]{3,2,1,0:T(8,128)(2,1)} %stack.3), calls=%async_computation.1 | async-start | bytes 1572864 | tf_op jit(solution)/shard_map/all_to_all | solution.py:52
  42.6 17.3 %all-to-all-done.1 = bf16[4,2,64,768]{3,2,1,0:T(8,128)(2,1)S(1)} async-done(((bf16[4,2,64,768]{3,2,1,0:T(8,128)(2,1)}), bf16[4,2,64,768]{3,2,1,0:T(8,128)(2,1)S(1)}, u32[]{:S(2)}, u32[]{:S(2)}) %all-to-all-start.1) | async-done | bytes 786464 | tf_op jit(solution)/shard_map/all_to_all | solution.py:52
  60.6 17.7 %all_gather.3 = bf16[2,256,768]{1,0,2:T(2,128)(2,1)S(1)} all-gather(bf16[2,256,192]{1,0,2:T(2,128)(2,1)S(1)} %copy.67), channel_id=1, replica_groups=mesh['dp'=8,'mp'=4] {'mp'}, dimensions={2}, use_global_device_ids=true | all-gather | bytes 983040 | tf_op jit(solution)/shard_map/all_gather | solution.py:64
  80.0 0.8 convolution_convert_fusion.2
  81.5 0.9 convolution_convert_fusion.3
  82.5 1.3 convolution_convert_fusion.1
  84.1 44.4 %all-reduce.4.cloned.1.call-done = bf16[2,256,768]{2,1,0:T(8,128)(2,1)} async-done(((bf16[2,256,768]{2,1,0:T(8,128)(2,1)}), bf16[2,256,768]{2,1,0:T(8,128)(2,1)}) %all-reduce.4.cloned.1.call-update) | async-done | bytes 786448 | tf_op jit(solution)/shard_map/psum | solution.py:83
  128.5 1.5 fusion.107
  130.4 1.3 fusion.63
  131.7 4.4 %convolution_convert_fusion = bf16[2,256,768]{2,1,0:T(8,128)(2,1)S(1)} fusion(bf16[768,768]{1,0:T(8,128)(2,1)S(1)} %copy-done.7, f32[2,256,768]{2,1,0:T(8,128)S(1)} %get-tuple-element.13, u8[256,768]{1,0:T(8,128)(4,1)S(1)} %get-tuple-element.6, u8[256,768]{1,0:T(8,128)(4,1)S(1)} %get-tuple-element.5), kind=kOutput, calls=%fused_computation.41 | convolution fusion | flops 631898112 | bytes 3932160 | tf_op jit(solution)/shard_map/btf,fd->btd/dot_general | solution.py:90
  136.1 1.7 copy.73
  139.1 42.0 %all-reduce.6.cloned.1.call-done = bf16[2,256,768]{2,0,1:T(2,128)(2,1)} async-done(((bf16[2,256,768]{2,0,1:T(2,128)(2,1)}), bf16[2,256,768]{2,0,1:T(2,128)(2,1)}) %all-reduce.6.cloned.1.call-update) | async-done | bytes 786448
  181.2 1.1 constant_dynamic-slice_fusion
  (56 shorter events, 8.3 us)
Async XLA Ops:
  6.5 123.8 %copy-start = (bf16[768,768]{1,0:T(8,128)(2,1)S(1)}, bf16[768,768]{1,0:T(8,128)(2,1)}, u32[]{:S(2)}) copy-start(bf16[768,768]{1,0:T(8,128)(2,1)} %param.22) | copy-start | bytes 3538948
  16.2 17.8 %all-to-all-start = ((bf16[8,2,24576]{2,1,0:T(2,128)(2,1)}), bf16[8,2,24576]{2,1,0:T(2,128)(2,1)S(1)}, u32[]{:S(2)}, u32[]{:S(2)}) async-start(bf16[8,2,24576]{2,1,0:T(2,128)(2,1)} %reshape.161), calls=%async_computation | async-start | bytes 1572864 | tf_op jit(solution)/shard_map/all_to_all | solution.py:45
  36.5 6.1 %copy-start.4 = (bf16[256,192]{0,1:T(8,128)(2,1)S(1)}, bf16[256,192]{0,1:T(8,128)(2,1)}, u32[]{:S(2)}) copy-start(bf16[256,192]{0,1:T(8,128)(2,1)} %param.17) | copy-start | bytes 294916
  36.5 6.1 %copy-start.5 = (bf16[768]{0:T(1024)(128)(2,1)S(1)}, bf16[768]{0:T(1024)(128)(2,1)}, u32[]{:S(2)}) copy-start(bf16[768]{0:T(1024)(128)(2,1)} %param.20) | copy-start | bytes 4612
  37.5 22.4 %copy-start.3 = (bf16[768,192]{0,1:T(8,128)(2,1)S(1)}, bf16[768,192]{0,1:T(8,128)(2,1)}, u32[]{:S(2)}) copy-start(bf16[768,192]{0,1:T(8,128)(2,1)} %param.16) | copy-start | bytes 884740
  37.5 22.4 %all-to-all-start.1 = ((bf16[4,2,64,768]{3,2,1,0:T(8,128)(2,1)}), bf16[4,2,64,768]{3,2,1,0:T(8,128)(2,1)S(1)}, u32[]{:S(2)}, u32[]{:S(2)}) async-start(bf16[4,2,64,768]{3,2,1,0:T(8,128)(2,1)} %stack.3), calls=%async_computation.1 | async-start | bytes 1572864 | tf_op jit(solution)/shard_map/all_to_all | solution.py:52
  42.5 85.9 %all-reduce.4.cloned.1.call-start = ((), (), s32[]{:S(2)}) async-start(), calls=%async_computation.2 | async-start | bytes 1572864 | tf_op jit(solution)/shard_map/psum | solution.py:83
  78.9 1.2 copy-start.8
  81.5 1.0 copy-start.2
  82.4 1.7 copy-start.6
  83.8 97.3 %all-reduce.6.cloned.1.call-start = ((), (), s32[]{:S(2)}) async-start(), calls=%async_computation.3 | async-start | bytes 1572864
  128.5 1.5 copy-start.1
  130.4 1.3 copy-start.7
  136.1 1.8 copy-start.9
Sparse Core Ops, SparseCore 0:
  84.0 44.4 all-reduce.3
  138.0 43.1 all-reduce.5
